TPU v7x, 32 devices: a whole 2x2x4 slice. The times are simulated.
32 devices in a mesh: seq: 8 (over z, x), head: 4 (over y, core).
Axes of the slice: x: 2, y: 2, z: 4, core: 2. Of those that a mesh axis runs over, the one named last changes fastest.
Arguments:
- q_latent: bfloat16 [2048, 1536], P('seq', 'head'), may hold values from -6 to 6
- kv_latent: bfloat16 [2048, 512], P('seq', 'head'), may hold values from -6 to 6
- k_rope: bfloat16 [2048, 64], P('seq'), may hold values from -6 to 6
- segment_ids: int32 [2048], P('seq'), may hold values from 0 to 7, as said below
- w_q_nope: bfloat16 [1536, 16384], P('seq', 'head'), may hold values from -6 to 6
- w_q_rope: bfloat16 [1536, 8192], P('seq', 'head'), may hold values from -6 to 6
- w_kv_nope: bfloat16 [512, 16384], P('seq', 'head'), may hold values from -6 to 6
- threshold: float32 [1], replicated, may hold values from 3.5 to 5.5
Outputs:
- new_q_nope: bfloat16 [1536, 16384], P('seq', 'head')
- new_q_rope: bfloat16 [1536, 8192], P('seq', 'head')
- new_kv_nope: bfloat16 [512, 16384], P('seq', 'head')
- head_max: float32 [128], P('head')
- row_max: float32 [2048, 128], P('seq', 'head')
Inputs may be any that keep to these rules, and one draw needn't show every extreme that they name: segment_ids never fall along the tokens and each document has 1 to 768 tokens.
All inputs are finite; a program needn't handle non-finite values.
Results may differ from a plain program's by a relative error of at most 0.0034.
Values may be sent and summed in bfloat16 or wider, within the bound.
A program may use at most 128 MiB of HBM per device.

v0:
```python
import math
import jax
import jax.numpy as jnp
from jax import lax
from jax.sharding import PartitionSpec as P

D_NOPE = 128
D_ROPE = 64
QLORA = 1536
KVLORA = 512
REACH = 3


def as_sent(value):
    return jax.tree.map(lambda a: a.astype(jnp.bfloat16) if a.dtype == jnp.float32 else a, value)


def from_partner(value, axis, stride):
    mask = 2**stride
    pairs = [(source, source ^ mask) for source in range(lax.axis_size(axis))]
    return lax.ppermute(value, axis, pairs)


def shifted(block, axis, distance):
    devices = range(lax.axis_size(axis))
    route = [(i - distance, i) for i in devices if i - distance in devices]
    return lax.ppermute(block, axis, route)


def score_max(query_nope, query_rope, key_nope, key_rope, allowed):
    nope = jnp.einsum("qhd,khd->hqk", query_nope, key_nope, preferred_element_type=jnp.float32)
    rope = jnp.einsum("qhd,kd->hqk", query_rope, key_rope, preferred_element_type=jnp.float32)
    scores = (nope + rope) * (1.0 / math.sqrt(D_NOPE + D_ROPE))
    return jnp.max(jnp.where(allowed[None], scores, jnp.float32(-1e30)), axis=2)


def masked_max(compute, operands):
    return compute(*operands)


def spread_columns(weight, width, quarter, copies):
    pieces = weight.reshape(weight.shape[0], 4, quarter * width).transpose(1, 0, 2)
    return jnp.tile(pieces, (copies, 1, 1))


def body(q_latent, kv_latent, k_rope, segment_ids, w_q_nope, w_q_rope, w_kv_nope, threshold):
    q_whole, kv_whole = (
        lax.all_gather(q_latent, "head", axis=1, tiled=True),
        lax.all_gather(kv_latent, "head", axis=1, tiled=True),
    )
    rows = q_whole.shape[0]
    heads = w_q_nope.shape[1] // D_NOPE
    q_scale = 1.0 / math.sqrt(QLORA)
    k_scale = 1.0 / math.sqrt(KVLORA)
    place = lax.axis_index("seq")
    quarter = heads // 4
    copies = lax.axis_size("seq") // 4
    slot = place % 4
    sent = (
        spread_columns(w_q_nope, D_NOPE, quarter, copies),
        spread_columns(w_q_rope, D_ROPE, quarter, copies),
        spread_columns(w_kv_nope, D_NOPE, quarter, copies),
    )
    got_nope, got_rope, got_kv = (
        lax.all_to_all(sent[0], "seq", split_axis=0, concat_axis=1, tiled=True),
        lax.all_to_all(sent[1], "seq", split_axis=0, concat_axis=1, tiled=True),
        lax.all_to_all(sent[2], "seq", split_axis=0, concat_axis=1, tiled=True),
    )
    sub_nope = got_nope.reshape(QLORA, quarter * D_NOPE)
    sub_rope = got_rope.reshape(QLORA, quarter * D_ROPE)
    sub_kv = got_kv.reshape(KVLORA, quarter * D_NOPE)
    group = (q_whole, kv_whole, k_rope)
    for level in range(2):
        partner = jax.tree.map(
            lambda part, own: part.astype(own.dtype),
            from_partner(as_sent(group), "seq", level),
            group,
        )
        upper = place // (1 << level) % 2 == 1
        group = tuple(
            (
                jnp.where(
                    upper, jnp.concatenate([other, mine], 0), jnp.concatenate([mine, other], 0)
                )
                for mine, other in zip(group, partner)
            )
        )
    group_q, group_kv, group_rope = group
    early_kv, early_rope = shifted(
        (group_kv[(4 - REACH) * rows :], group_rope[(4 - REACH) * rows :]), "seq", 4
    )
    keys_kv = jnp.concatenate([early_kv, group_kv], 0)
    keys_rope = jnp.concatenate([early_rope, group_rope], 0)
    key_nope = (
        (jnp.dot(keys_kv, sub_kv, preferred_element_type=jnp.float32) * k_scale)
        .astype(jnp.bfloat16)
        .reshape(keys_kv.shape[0], quarter, D_NOPE)
    )
    query_nope = (
        (jnp.dot(group_q, sub_nope, preferred_element_type=jnp.float32) * q_scale)
        .astype(jnp.bfloat16)
        .reshape(4 * rows, quarter, D_NOPE)
    )
    query_rope = (
        (jnp.dot(group_q, sub_rope, preferred_element_type=jnp.float32) * q_scale)
        .astype(jnp.bfloat16)
        .reshape(4 * rows, quarter, D_ROPE)
    )
    all_segs = lax.all_gather(segment_ids, "seq", axis=0, tiled=True)
    padded_segs = jnp.concatenate([jnp.full((REACH * rows,), -1, jnp.int32), all_segs], 0)
    first = place // 4 * 4
    window = (REACH + 1) * rows
    block_rows = []
    for local in range(4):
        block = first + local
        query_seg = lax.dynamic_slice_in_dim(all_segs, block * rows, rows, 0)
        key_seg = lax.dynamic_slice_in_dim(padded_segs, block * rows, window, 0)
        query_pos = block * rows + jnp.arange(rows, dtype=jnp.int32)
        key_pos = (block - REACH) * rows + jnp.arange(window, dtype=jnp.int32)
        allowed = (
            (query_seg[:, None] == key_seg[None, :])
            & (key_pos[None, :] <= query_pos[:, None])
            & (key_pos[None, :] >= 0)
        )
        operands = (
            query_nope[local * rows : (local + 1) * rows],
            query_rope[local * rows : (local + 1) * rows],
            key_nope[local * rows : local * rows + window],
            keys_rope[local * rows : local * rows + window],
            allowed,
        )
        block_rows.append(masked_max(score_max, operands))
    stacked = jnp.stack(block_rows, 0)[None]
    for level in range(2):
        partner = from_partner(stacked, "seq", level)
        upper = place // (1 << level) % 2 == 1
        stacked = jnp.where(
            upper, jnp.concatenate([partner, stacked], 0), jnp.concatenate([stacked, partner], 0)
        )
    own = lax.dynamic_index_in_dim(stacked, slot, 1, False)
    row_max = own.reshape(heads, rows).T
    local_heads = jnp.max(row_max, axis=0)
    head_max = lax.pmax(local_heads, "seq")
    clip = threshold[0] / jnp.maximum(head_max, threshold[0])
    root = jnp.sqrt(clip)
    new_q_nope = (w_q_nope.astype(jnp.float32) * jnp.repeat(root, D_NOPE)[None, :]).astype(
        jnp.bfloat16
    )
    new_q_rope = (w_q_rope.astype(jnp.float32) * jnp.repeat(clip, D_ROPE)[None, :]).astype(
        jnp.bfloat16
    )
    new_kv_nope = (w_kv_nope.astype(jnp.float32) * jnp.repeat(root, D_NOPE)[None, :]).astype(
        jnp.bfloat16
    )
    return (new_q_nope, new_q_rope, new_kv_nope, head_max, row_max)


def solution(mesh):
    in_specs = (
        P("seq", "head"),
        P("seq", "head"),
        P("seq", None),
        P("seq"),
        P("seq", "head"),
        P("seq", "head"),
        P("seq", "head"),
        P(),
    )
    out_specs = (P("seq", "head"), P("seq", "head"), P("seq", "head"), P("head"), P("seq", "head"))
    return jax.shard_map(body, mesh=mesh, in_specs=in_specs, out_specs=out_specs, check_vma=False)
```

profile of v0, /device:TPU:0, one launch (start us, length us, event | category | flops | bytes accessed | tf_op | source)
XLA Modules:
  0.0 299.3 jit_solution(7385676597361516628)
XLA Ops:
  0.6 1.5 reshape.406
  2.2 0.2 copy.29
  2.3 1.1 tile.14
  3.4 7.3 %all-to-all-start.1 = ((bf16[8,64,1024]{2,1,0:T(8,128)(2,1)}), bf16[8,64,1024]{2,1,0:T(8,128)(2,1)S(1)}, u32[]{:S(2)}, u32[]{:S(2)}) async-start(bf16[8,64,1024]{2,1,0:T(8,128)(2,1)} %bitcast.8), calls=%async_computation.1 | async-start | bytes 2097152 | tf_op jit(solution)/shard_map/all_to_all | solution.py:67
  10.7 0.6 reshape.408
  11.3 0.1 copy.32
  11.4 25.0 %all-to-all-done.1 = bf16[8,64,1024]{2,1,0:T(8,128)(2,1)S(1)} async-done(((bf16[8,64,1024]{2,1,0:T(8,128)(2,1)}), bf16[8,64,1024]{2,1,0:T(8,128)(2,1)S(1)}, u32[]{:S(2)}, u32[]{:S(2)}) %all-to-all-start.1) | async-done | bytes 1048608 | tf_op jit(solution)/shard_map/all_to_all | solution.py:67
  36.5 1.4 tile.31
  37.9 4.3 %all-to-all-start.2 = ((bf16[8,192,512]{2,1,0:T(8,128)(2,1)}), bf16[8,192,512]{2,1,0:T(8,128)(2,1)}, u32[]{:S(2)}, u32[]{:S(2)}) async-start(bf16[8,192,512]{2,1,0:T(8,128)(2,1)} %bitcast.13), calls=%async_computation.2 | async-start | bytes 3145728 | tf_op jit(solution)/shard_map/all_to_all | solution.py:66
  42.3 1.2 reshape.404
  43.5 0.5 copy.28
  43.9 34.9 %all-to-all-done.2 = bf16[8,192,512]{2,1,0:T(8,128)(2,1)} async-done(((bf16[8,192,512]{2,1,0:T(8,128)(2,1)}), bf16[8,192,512]{2,1,0:T(8,128)(2,1)}, u32[]{:S(2)}, u32[]{:S(2)}) %all-to-all-start.2) | async-done | bytes 1572896 | tf_op jit(solution)/shard_map/all_to_all | solution.py:66
  78.8 2.1 tile.12
  81.0 4.6 %all-to-all-start = ((bf16[8,192,1024]{2,1,0:T(8,128)(2,1)}), bf16[8,192,1024]{2,1,0:T(8,128)(2,1)}, u32[]{:S(2)}, u32[]{:S(2)}) async-start(bf16[8,192,1024]{2,1,0:T(8,128)(2,1)} %bitcast.4), calls=%async_computation | async-start | bytes 6291456 | tf_op jit(solution)/shard_map/all_to_all | solution.py:65
  85.6 1.9 collective-permute-start.5
  87.5 5.8 %all_gather.11 = bf16[256,512]{1,0:T(8,128)(2,1)S(1)} all-gather(bf16[256,128]{1,0:T(8,128)(2,1)S(1)} %copy-done.15), channel_id=1, replica_groups=mesh['seq'=8,'head'=4] {'head'}, dimensions={1}, use_global_device_ids=true | all-gather | bytes 327680 | tf_op jit(solution)/shard_map/all_gather | solution.py:49
  93.3 0.2 collective-permute-start.2
  93.5 8.6 %all_gather.10 = bf16[256,1536]{1,0:T(8,128)(2,1)S(1)} all-gather(bf16[256,384]{1,0:T(8,128)(2,1)S(1)} %copy-done.14), channel_id=1, replica_groups=mesh['seq'=8,'head'=4] {'head'}, dimensions={1}, use_global_device_ids=true | all-gather | bytes 983040 | tf_op jit(solution)/shard_map/all_gather | solution.py:48
  102.1 1.8 collective-permute-start
  104.0 50.2 %all-gather = s32[8,1,256]{2,1,0:T(1,128)S(1)} all-gather(s32[1,1,256]{2,1,0:T(1,128)S(1)} %bitcast.118), channel_id=1, replica_groups=mesh['seq'=8,'head'=4] {'seq'}, dimensions={0}, use_global_device_ids=true | all-gather | bytes 9216 | tf_op jit(solution)/shard_map/all_gather | solution.py:109
  154.2 0.1 fusion.40
  154.3 0.1 pad_dynamic-slice_fusion.7
  154.4 0.2 maximum_select_fusion.5
  154.6 11.1 %collective-permute-start.3 = (bf16[512,512]{1,0:T(8,128)(2,1)S(1)}, bf16[512,512]{1,0:T(8,128)(2,1)S(1)}, u32[]{:S(2)}, u32[]{:S(2)}) collective-permute-start(bf16[512,512]{1,0:T(8,128)(2,1)S(1)} %maximum_select_fusion.5), channel_id=1, source_target_pairs={{0,8},{4,12},{8,0},{12,4},{16,24},{20,28},{24,16},{28,20},{1,9},{5... | collective-permute-start | bytes 1572872 | tf_op jit(solution)/shard_map/ppermute | solution.py:21
  165.7 0.3 and_and_fusion.3
  166.0 1.2 and_and_fusion.1
  167.3 6.2 %collective-permute-done.3 = bf16[512,512]{1,0:T(8,128)(2,1)S(1)} collective-permute-done((bf16[512,512]{1,0:T(8,128)(2,1)S(1)}, bf16[512,512]{1,0:T(8,128)(2,1)S(1)}, u32[]{:S(2)}, u32[]{:S(2)}) %collective-permute-start.3) | collective-permute-done | bytes 524320 | tf_op jit(solution)/shard_map/ppermute | solution.py:21
  173.5 0.5 maximum_select_fusion.2
  174.1 4.7 %collective-permute-start.4 = (bf16[768,512]{1,0:T(8,128)(2,1)S(1)}, bf16[768,512]{1,0:T(8,128)(2,1)S(1)}, u32[]{:S(2)}, u32[]{:S(2)}) collective-permute-start(bf16[768,512]{1,0:T(8,128)(2,1)S(1)} %slice.117), channel_id=1, source_target_pairs={{0,16},{4,20},{8,24},{12,28},{1,17},{5,21},{9,25},{13,29},{2,18},{... | collective-permute-start | bytes 2359304 | tf_op jit(solution)/shard_map/ppermute | solution.py:27
  178.8 0.6 maximum_select_fusion.1
  179.4 0.6 collective-permute-start.1
  180.1 1.5 collective-permute-start.6
  181.6 0.3 and_and_fusion
  182.0 44.8 %collective-permute-done.6 = bf16[512,64]{0,1:T(8,128)(2,1)S(1)} collective-permute-done((bf16[512,64]{0,1:T(8,128)(2,1)S(1)}, bf16[512,64]{0,1:T(8,128)(2,1)S(1)}, u32[]{:S(2)}, u32[]{:S(2)}) %collective-permute-start.6) | collective-permute-done | bytes 65568 | tf_op jit(solution)/shard_map/ppermute | solution.py:21
  226.8 0.6 slice.119
  227.4 2.1 collective-permute-start.7
  229.6 2.2 multiply_convert_fusion
  231.8 3.0 fusion.37
  234.7 3.9 %multiply_convert_fusion.3 = bf16[1024,512]{0,1:T(8,128)(2,1)S(1)} fusion(bf16[1536,512]{1,0:T(8,128)(2,1)} %bitcast.14, bf16[512,1536]{1,0:T(8,128)(2,1)S(1)} %maximum_select_fusion.1, bf16[512,1536]{1,0:T(8,128)(2,1)S(1)} %collective-permute-done.1, pred[]{:T(512)S(6)} %eq.82), kind=kOutput, calls=%fused_computation.20 | convolution fusion | flops 1625817088 | bytes 5767169 | tf_op jit(solution)/shard_map/dot_general | solution.py:105
  238.6 0.9 fusion.39
  239.5 7.3 %multiply_convert_fusion.1 = bf16[1024,1024]{0,1:T(8,128)(2,1)S(1)} fusion(bf16[1536,1024]{1,0:T(8,128)(2,1)} %bitcast.5, bf16[512,1536]{1,0:T(8,128)(2,1)} %copy-done.8, bf16[512,1536]{1,0:T(8,128)(2,1)} %copy-done.19, pred[]{:T(512)S(6)} %eq.82), kind=kOutput, calls=%fused_computation.17 | convolution fusion | flops 3237478400 | bytes 8388609 | tf_op jit(solution)/shard_map/dot_general | solution.py:100
  246.8 0.1 fusion.38
  246.9 1.4 copy-done.2
  248.4 1.3 fusion.44
  249.7 0.3 copy-done.1
  250.0 1.3 fusion.41
  251.2 0.3 copy-done
  251.5 1.3 fusion.43
  252.9 2.1 fusion.2
  255.0 1.5 fusion.42
  256.5 3.0 %fusion.11 = f32[8,256]{1,0:T(8,128)S(1)} fusion(f32[8,256,1024]{2,1,0:T(8,128)S(1)} %fusion.41, pred[256,1024]{1,0:T(8,128)(4,1)S(1)} %and_and_fusion.3, bf16[256,8,64]{0,2,1:T(8,128)(2,1)S(1)} %bitcast.109, bf16[1024,64]{0,1:T(8,128)(2,1)S(1)} %maximum_select_fusion.6, bf16[768,64]{0,1:T(8,128)(2,1)} %collective-permute-done.7), kind=kOutput, calls=%fused_computation.15 | convolution fusion | flops 277084160 | bytes 9150464 | tf_op jit(solution)/shard_map/qhd,kd->hqk/dot_general | solution.py:32
  259.6 2.9 fusion.5
  262.5 3.1 %fusion.8 = f32[8,256]{1,0:T(8,128)S(1)} fusion(f32[8,256,1024]{2,1,0:T(8,128)S(1)} %fusion.42, pred[256,1024]{1,0:T(8,128)(4,1)S(1)} %get-tuple-element.30, bf16[256,8,64]{0,2,1:T(8,128)(2,1)S(1)} %bitcast.107, bf16[1024,64]{0,1:T(8,128)(2,1)S(1)} %maximum_select_fusion.6, bf16[768,64]{0,1:T(8,128)(2,1)} %collective-permute-done.7), kind=kOutput, calls=%fused_computation.11 | convolution fusion | flops 277084160 | bytes 9150464 | tf_op jit(solution)/shard_map/qhd,kd->hqk/dot_general | solution.py:32
  265.7 3.4 %collective-permute-start.8 = (f32[1,4,8,256]{3,2,0,1:T(8,128)S(1)}, f32[1,4,8,256]{3,2,0,1:T(8,128)S(1)}, u32[]{:S(2)}, u32[]{:S(2)}) collective-permute-start(f32[1,4,8,256]{3,2,0,1:T(8,128)S(1)} %maximum_bitcast_fusion), channel_id=1, source_target_pairs={{0,4},{4,0},{8,12},{12,8},{16,20},{20,16},{24,28},{28,24},{1,5},{5... | collective-permute-start | bytes 98312 | tf_op jit(solution)/shard_map/ppermute | solution.py:21
  269.1 1.9 collective-permute-done.8
  271.0 2.5 collective-permute-start.9
  274.2 1.6 collective-permute-done.9
  275.8 0.6 fusion.35
  276.4 0.1 reduce_max.52
  276.5 19.1 %pmax.7 = f32[32]{0:T(128)S(1)} all-reduce(f32[32]{0:T(128)S(1)} %reduce_max.52), channel_id=1, replica_groups=mesh['seq'=8,'head'=4] {'seq'}, use_global_device_ids=true, to_apply=%region_5.6 | all-reduce | flops 32 | bytes 256 | tf_op jit(solution)/shard_map/pmax | solution.py:143
  295.7 0.1 broadcast_bitcast_fusion
  295.7 0.9 multiply_convert_fusion.5
  296.6 1.5 multiply_convert_fusion.2
  298.2 1.0 multiply_convert_fusion.4
  (64 shorter events, 0.5 us)
Async XLA Ops:
  0.6 10.1 %copy-start.5 = (bf16[192,2048]{1,0:T(8,128)(2,1)S(1)}, bf16[192,2048]{1,0:T(8,128)(2,1)}, u32[]{:S(2)}) copy-start(bf16[192,2048]{1,0:T(8,128)(2,1)} %param.13) | copy-start | bytes 2359300
  3.4 33.0 %all-to-all-start.1 = ((bf16[8,64,1024]{2,1,0:T(8,128)(2,1)}), bf16[8,64,1024]{2,1,0:T(8,128)(2,1)S(1)}, u32[]{:S(2)}, u32[]{:S(2)}) async-start(bf16[8,64,1024]{2,1,0:T(8,128)(2,1)} %bitcast.8), calls=%async_computation.1 | async-start | bytes 2097152 | tf_op jit(solution)/shard_map/all_to_all | solution.py:67
  11.4 30.8 %copy-start.3 = (bf16[192,4096]{1,0:T(8,128)(2,1)S(1)}, bf16[192,4096]{1,0:T(8,128)(2,1)}, u32[]{:S(2)}) copy-start(bf16[192,4096]{1,0:T(8,128)(2,1)} %param.12) | copy-start | bytes 4718596
  36.5 1.5 copy-start.9
  37.9 40.9 %all-to-all-start.2 = ((bf16[8,192,512]{2,1,0:T(8,128)(2,1)}), bf16[8,192,512]{2,1,0:T(8,128)(2,1)}, u32[]{:S(2)}, u32[]{:S(2)}) async-start(bf16[8,192,512]{2,1,0:T(8,128)(2,1)} %bitcast.13), calls=%async_computation.2 | async-start | bytes 3145728 | tf_op jit(solution)/shard_map/all_to_all | solution.py:66
  80.9 4.6 %copy-start.16 = (bf16[256,64]{0,1:T(8,128)(2,1)S(1)}, bf16[256,64]{0,1:T(8,128)(2,1)}, u32[]{:S(2)}) copy-start(bf16[256,64]{0,1:T(8,128)(2,1)} %param.10) | copy-start | bytes 98308
  80.9 6.5 %copy-start.15 = (bf16[256,128]{1,0:T(8,128)(2,1)S(1)}, bf16[256,128]{1,0:T(8,128)(2,1)}, u32[]{:S(2)}) copy-start(bf16[256,128]{1,0:T(8,128)(2,1)} %param.9) | copy-start | bytes 196612
  80.9 12.5 %copy-start.14 = (bf16[256,384]{1,0:T(8,128)(2,1)S(1)}, bf16[256,384]{1,0:T(8,128)(2,1)}, u32[]{:S(2)}) copy-start(bf16[256,384]{1,0:T(8,128)(2,1)} %param.8) | copy-start | bytes 589828
  81.0 23.1 %copy-start.17 = (s32[256]{0:T(256)S(1)}, s32[256]{0:T(256)}, u32[]{:S(2)}) copy-start(s32[256]{0:T(256)} %param.11) | copy-start | bytes 3076
  81.0 158.5 %all-to-all-start = ((bf16[8,192,1024]{2,1,0:T(8,128)(2,1)}), bf16[8,192,1024]{2,1,0:T(8,128)(2,1)}, u32[]{:S(2)}, u32[]{:S(2)}) async-start(bf16[8,192,1024]{2,1,0:T(8,128)(2,1)} %bitcast.4), calls=%async_computation | async-start | bytes 6291456 | tf_op jit(solution)/shard_map/all_to_all | solution.py:65
  85.6 94.5 %collective-permute-start.5 = (bf16[256,64]{0,1:T(8,128)(2,1)S(1)}, bf16[256,64]{0,1:T(8,128)(2,1)S(1)}, u32[]{:S(2)}, u32[]{:S(2)}) collective-permute-start(bf16[256,64]{0,1:T(8,128)(2,1)S(1)} %copy-done.16), channel_id=1, source_target_pairs={{0,4},{4,0},{8,12},{12,8},{16,20},{20,16},{24,28},{28,24},{1,5},{5... | collective-permute-start | bytes 98312 | tf_op jit(solution)/shard_map/ppermute | solution.py:21
  93.3 61.1 %collective-permute-start.2 = (bf16[256,512]{1,0:T(8,128)(2,1)S(1)}, bf16[256,512]{1,0:T(8,128)(2,1)S(1)}, u32[]{:S(2)}, u32[]{:S(2)}) collective-permute-start(bf16[256,512]{1,0:T(8,128)(2,1)S(1)} %all_gather.11), channel_id=1, source_target_pairs={{0,4},{4,0},{8,12},{12,8},{16,20},{20,16},{24,28},{28,24},{1,5},{5... | collective-permute-start | bytes 786440 | tf_op jit(solution)/shard_map/ppermute | solution.py:21
  102.1 76.7 %collective-permute-start = (bf16[256,1536]{1,0:T(8,128)(2,1)S(1)}, bf16[256,1536]{1,0:T(8,128)(2,1)S(1)}, u32[]{:S(2)}, u32[]{:S(2)}) collective-permute-start(bf16[256,1536]{1,0:T(8,128)(2,1)S(1)} %all_gather.10), channel_id=1, source_target_pairs={{0,4},{4,0},{8,12},{12,8},{16,20},{20,16},{24,28},{28,24},{1,5},{5... | collective-permute-start | bytes 2359304 | tf_op jit(solution)/shard_map/ppermute | solution.py:21
  154.6 18.9 %collective-permute-start.3 = (bf16[512,512]{1,0:T(8,128)(2,1)S(1)}, bf16[512,512]{1,0:T(8,128)(2,1)S(1)}, u32[]{:S(2)}, u32[]{:S(2)}) collective-permute-start(bf16[512,512]{1,0:T(8,128)(2,1)S(1)} %maximum_select_fusion.5), channel_id=1, source_target_pairs={{0,8},{4,12},{8,0},{12,4},{16,24},{20,28},{24,16},{28,20},{1,9},{5... | collective-permute-start | bytes 1572872 | tf_op jit(solution)/shard_map/ppermute | solution.py:21
  174.0 55.6 %copy-start.10 = (bf16[8,64,1024]{2,1,0:T(8,128)(2,1)S(1)}, bf16[8,64,1024]{2,1,0:T(8,128)(2,1)}, u32[]{:S(2)}) copy-start(bf16[8,64,1024]{2,1,0:T(8,128)(2,1)} %copy-done.9) | copy-start | bytes 3145732
  174.1 55.5 %collective-permute-start.4 = (bf16[768,512]{1,0:T(8,128)(2,1)S(1)}, bf16[768,512]{1,0:T(8,128)(2,1)S(1)}, u32[]{:S(2)}, u32[]{:S(2)}) collective-permute-start(bf16[768,512]{1,0:T(8,128)(2,1)S(1)} %slice.117), channel_id=1, source_target_pairs={{0,16},{4,20},{8,24},{12,28},{1,17},{5,21},{9,25},{13,29},{2,18},{... | collective-permute-start | bytes 2359304 | tf_op jit(solution)/shard_map/ppermute | solution.py:27
  179.4 55.3 %copy-start.8 = (bf16[512,1536]{1,0:T(8,128)(2,1)}, bf16[512,1536]{1,0:T(8,128)(2,1)S(1)}, u32[]{:S(2)}) copy-start(bf16[512,1536]{1,0:T(8,128)(2,1)S(1)} %maximum_select_fusion.1) | copy-start | bytes 4718596
  179.4 55.3 %collective-permute-start.1 = (bf16[512,1536]{1,0:T(8,128)(2,1)S(1)}, bf16[512,1536]{1,0:T(8,128)(2,1)S(1)}, u32[]{:S(2)}, u32[]{:S(2)}) collective-permute-start(bf16[512,1536]{1,0:T(8,128)(2,1)S(1)} %maximum_select_fusion.1), channel_id=1, source_target_pairs={{0,8},{4,12},{8,0},{12,4},{16,24},{20,28},{24,16},{28,20},{1,9},{5... | collective-permute-start | bytes 4718600 | tf_op jit(solution)/shard_map/ppermute | solution.py:21
  180.1 46.6 %collective-permute-start.6 = (bf16[512,64]{0,1:T(8,128)(2,1)S(1)}, bf16[512,64]{0,1:T(8,128)(2,1)S(1)}, u32[]{:S(2)}, u32[]{:S(2)}) collective-permute-start(bf16[512,64]{0,1:T(8,128)(2,1)S(1)} %maximum_select_fusion.7), channel_id=1, source_target_pairs={{0,8},{4,12},{8,0},{12,4},{16,24},{20,28},{24,16},{28,20},{1,9},{5... | collective-permute-start | bytes 196616 | tf_op jit(solution)/shard_map/ppermute | solution.py:21
  227.4 29.1 %collective-permute-start.7 = (bf16[768,64]{0,1:T(8,128)(2,1)}, bf16[768,64]{0,1:T(8,128)(2,1)}, u32[]{:S(2)}, u32[]{:S(2)}) collective-permute-start(bf16[768,64]{0,1:T(8,128)(2,1)} %slice.119), channel_id=1, source_target_pairs={{0,16},{4,20},{8,24},{12,28},{1,17},{5,21},{9,25},{13,29},{2,18},{... | collective-permute-start | bytes 294920 | tf_op jit(solution)/shard_map/ppermute | solution.py:27
  234.7 3.9 %copy-start.19 = (bf16[512,1536]{1,0:T(8,128)(2,1)}, bf16[512,1536]{1,0:T(8,128)(2,1)S(1)}, u32[]{:S(2)}) copy-start(bf16[512,1536]{1,0:T(8,128)(2,1)S(1)} %collective-permute-done.1) | copy-start | bytes 4718596
  246.8 1.6 copy-start.2
  248.4 1.6 copy-start.1
  250.0 1.6 copy-start
  251.5 1.3 copy-start.13
  256.5 3.1 %copy-start.11 = (pred[256,1024]{1,0:T(8,128)(4,1)S(1)}, pred[256,1024]{1,0:T(8,128)(4,1)}, u32[]{:S(2)}) copy-start(pred[256,1024]{1,0:T(8,128)(4,1)} %get-tuple-element.29) | copy-start | bytes 786436
  259.6 2.9 copy-start.12
  262.5 33.2 %copy-start.7 = (bf16[64,4096]{1,0:T(8,128)(2,1)S(1)}, bf16[64,4096]{1,0:T(8,128)(2,1)}, u32[]{:S(2)}) copy-start(bf16[64,4096]{1,0:T(8,128)(2,1)} %param.14) | copy-start | bytes 1572868
  262.5 34.1 %copy-start.4 = (bf16[192,4096]{1,0:T(8,128)(2,1)S(1)}, bf16[192,4096]{1,0:T(8,128)(2,1)}, u32[]{:S(2)}) copy-start(bf16[192,4096]{1,0:T(8,128)(2,1)} %param.12) | copy-start | bytes 4718596
  265.7 32.6 %copy-start.6 = (bf16[192,2048]{1,0:T(8,128)(2,1)S(1)}, bf16[192,2048]{1,0:T(8,128)(2,1)}, u32[]{:S(2)}) copy-start(bf16[192,2048]{1,0:T(8,128)(2,1)} %param.13) | copy-start | bytes 2359300
  265.7 5.3 %collective-permute-start.8 = (f32[1,4,8,256]{3,2,0,1:T(8,128)S(1)}, f32[1,4,8,256]{3,2,0,1:T(8,128)S(1)}, u32[]{:S(2)}, u32[]{:S(2)}) collective-permute-start(f32[1,4,8,256]{3,2,0,1:T(8,128)S(1)} %maximum_bitcast_fusion), channel_id=1, source_target_pairs={{0,4},{4,0},{8,12},{12,8},{16,20},{20,16},{24,28},{28,24},{1,5},{5... | collective-permute-start | bytes 98312 | tf_op jit(solution)/shard_map/ppermute | solution.py:21
  271.0 4.8 %collective-permute-start.9 = (f32[2,4,8,256]{3,2,0,1:T(8,128)S(1)}, f32[2,4,8,256]{3,2,0,1:T(8,128)S(1)}, u32[]{:S(2)}, u32[]{:S(2)}) collective-permute-start(f32[2,4,8,256]{3,2,0,1:T(8,128)S(1)} %maximum_select_fusion.8), channel_id=1, source_target_pairs={{0,8},{4,12},{8,0},{12,4},{16,24},{20,28},{24,16},{28,20},{1,9},{5... | collective-permute-start | bytes 196616 | tf_op jit(solution)/shard_map/ppermute | solution.py:21
  295.6 3.6 %copy-start.18 = (f32[32]{0:T(128)}, f32[32]{0:T(128)S(1)}, u32[]{:S(2)}) copy-start(f32[32]{0:T(128)S(1)} %pmax.7) | copy-start | bytes 388
where the time goes:
time: 300 us; the launch traced here: 299 us
  waiting for transfers between devices  114 us (38%)
  blocking collectives  83.7 us (28%)
  starting transfers between devices  46.2 us (15%)
  matrix products  29.9 us (10%)
  local copies, waits for them, and re-layouts  16 us (5%)
  other arithmetic  7.27 us (2%)
    ppermute x8, waiting for transfers between devices, from_partner(): return lax.ppermute(value, axis, pairs)  54.5 us
    all_gather x1, blocking collectives, body(): all_segs = lax.all_gather(segment_ids, 'seq', axis=0, tiled=True)  50.2 us
    all_to_all x1, waiting for transfers between devices, body(): lax.all_to_all(sent[1], 'seq', split_axis=0, concat_axis=1, tiled=True)  34.9 us
    all_to_all x1, waiting for transfers between devices, body(): lax.all_to_all(sent[2], 'seq', split_axis=0, concat_axis=1, tiled=True)  25 us
    ppermute x8, starting transfers between devices, from_partner(): return lax.ppermute(value, axis, pairs)  23.1 us
    pmax x1, blocking collectives, body(): head_max = lax.pmax(local_heads, 'seq')  19.1 us
    dot_general x4, matrix products, score_max(): jnp.einsum('qhd,kd->hqk', query_rope, key_rope, preferred_element_type=jn...  11.2 us
    all_gather x1, blocking collectives, body(): lax.all_gather(q_latent, 'head', axis=1, tiled=True)  8.59 us
  transfers between devices with their start and end apart: 13, of which 6 were waited for; matrix products, arithmetic and copies ran while one was open for 10% of the time, Pallas kernels for 0%

commit v1 on v0

--- a/solution.py
+++ b/solution.py
@@ -106,7 +106,10 @@
         .astype(jnp.bfloat16)
         .reshape(4 * rows, quarter, D_ROPE)
     )
-    all_segs = lax.all_gather(segment_ids, "seq", axis=0, tiled=True)
+    peers = lax.axis_size("seq")
+    parts = jnp.stack([segment_ids for _ in range(peers)])
+    parts = lax.all_to_all(parts, "seq", split_axis=0, concat_axis=0)
+    all_segs = jnp.concatenate(parts, axis=0)
     padded_segs = jnp.concatenate([jnp.full((REACH * rows,), -1, jnp.int32), all_segs], 0)
     first = place // 4 * 4
     window = (REACH + 1) * rows

time: 300 us -> 287 us (0.957)
  blocking collectives: 83.7 us -> 32.2 us
  waiting for transfers between devices: 114 us -> 158 us
  starting transfers between devices: 46.2 us -> 41.1 us
    all_gather x1 -> x0, blocking collectives: 50.2 us -> none  [body(): all_segs = lax.all_gather(segment_ids, 'seq', axis=0, tiled=True)]
    ppermute x8, waiting for transfers between devices: 54.5 us -> 94.2 us  [from_partner(): return lax.ppermute(value, axis, pairs)]
    ppermute x8, starting transfers between devices: 23.1 us -> 9.44 us  [from_partner(): return lax.ppermute(value, axis, pairs)]
    all_to_all x0 -> x1, starting transfers between devices: none -> 7.28 us  [body(): parts = lax.all_to_all(parts, 'seq', split_axis=0, concat_axis=0)]
    ppermute x2, starting transfers between devices: 6.85 us -> 11.9 us  [shifted(): return lax.ppermute(block, axis, route)]
    all_to_all x0 -> x1, waiting for transfers between devices: none -> 4.92 us  [body(): parts = lax.all_to_all(parts, 'seq', split_axis=0, concat_axis=0)]
    all_to_all x1, starting transfers between devices: 7.28 us -> 3.56 us  [body(): lax.all_to_all(sent[2], 'seq', split_axis=0, concat_axis=1, tiled=True)]
  transfers between devices with their start and end apart: 13 -> 14, of which waited for: 6 -> 8; matrix products, arithmetic and copies ran while one was open for 10% -> 11% of each run, Pallas kernels for 0% -> 0%
where the time goes in v1:
time: 287 us
  waiting for transfers between devices  158 us (55%)
  starting transfers between devices  41.1 us (14%)
  blocking collectives  32.2 us (11%)
  matrix products  29.9 us (10%)
  local copies, waits for them, and re-layouts  17.3 us (6%)
  other arithmetic  6.63 us (2%)
    ppermute x8, waiting for transfers between devices, from_partner(): return lax.ppermute(value, axis, pairs)  94.2 us
    all_to_all x1, waiting for transfers between devices, body(): lax.all_to_all(sent[1], 'seq', split_axis=0, concat_axis=1, tiled=True)  34.7 us
    all_to_all x1, waiting for transfers between devices, body(): lax.all_to_all(sent[2], 'seq', split_axis=0, concat_axis=1, tiled=True)  24 us
    pmax x1, blocking collectives, body(): head_max = lax.pmax(local_heads, 'seq')  17.8 us
    ppermute x2, starting transfers between devices, shifted(): return lax.ppermute(block, axis, route)  11.9 us
    dot_general x4, matrix products, score_max(): jnp.einsum('qhd,kd->hqk', query_rope, key_rope, preferred_element_type=jn...  11.2 us
    ppermute x8, starting transfers between devices, from_partner(): return lax.ppermute(value, axis, pairs)  9.44 us
    all_gather x1, blocking collectives, body(): lax.all_gather(q_latent, 'head', axis=1, tiled=True)  8.59 us
  transfers between devices with their start and end apart: 14, of which 8 were waited for; matrix products, arithmetic and copies ran while one was open for 11% of the time, Pallas kernels for 0%

profile of v1, /device:TPU:0, one launch (start us, length us, event | category | flops | bytes accessed | tf_op | source)
XLA Modules:
  0.0 286.7 jit_solution(16926881100023622073)
XLA Ops:
  0.6 1.4 stack.12
  2.0 7.3 %all-to-all-start = ((s32[8,1,256]{2,1,0:T(1,128)}), s32[8,1,256]{2,1,0:T(1,128)S(1)}, u32[]{:S(2)}, u32[]{:S(2)}) async-start(s32[8,1,256]{2,1,0:T(1,128)} %stack.12), calls=%async_computation | async-start | bytes 16384 | tf_op jit(solution)/shard_map/all_to_all | solution.py:111
  9.3 1.4 reshape.418
  10.7 0.2 copy.14
  10.9 4.9 %all-to-all-done = s32[8,1,256]{2,1,0:T(1,128)S(1)} async-done(((s32[8,1,256]{2,1,0:T(1,128)}), s32[8,1,256]{2,1,0:T(1,128)S(1)}, u32[]{:S(2)}, u32[]{:S(2)}) %all-to-all-start) | async-done | bytes 8224 | tf_op jit(solution)/shard_map/all_to_all | solution.py:111
  15.8 1.1 tile.14
  16.9 3.6 %all-to-all-start.2 = ((bf16[8,64,1024]{2,1,0:T(8,128)(2,1)}), bf16[8,64,1024]{2,1,0:T(8,128)(2,1)S(1)}, u32[]{:S(2)}, u32[]{:S(2)}) async-start(bf16[8,64,1024]{2,1,0:T(8,128)(2,1)} %bitcast.7), calls=%async_computation.2 | async-start | bytes 2097152 | tf_op jit(solution)/shard_map/all_to_all | solution.py:67
  20.5 0.6 reshape.420
  21.1 0.1 copy.17
  21.2 24.0 %all-to-all-done.2 = bf16[8,64,1024]{2,1,0:T(8,128)(2,1)S(1)} async-done(((bf16[8,64,1024]{2,1,0:T(8,128)(2,1)}), bf16[8,64,1024]{2,1,0:T(8,128)(2,1)S(1)}, u32[]{:S(2)}, u32[]{:S(2)}) %all-to-all-start.2) | async-done | bytes 1048608 | tf_op jit(solution)/shard_map/all_to_all | solution.py:67
  45.2 1.4 tile.31
  46.7 4.3 %all-to-all-start.3 = ((bf16[8,192,512]{2,1,0:T(8,128)(2,1)}), bf16[8,192,512]{2,1,0:T(8,128)(2,1)}, u32[]{:S(2)}, u32[]{:S(2)}) async-start(bf16[8,192,512]{2,1,0:T(8,128)(2,1)} %bitcast.12), calls=%async_computation.3 | async-start | bytes 3145728 | tf_op jit(solution)/shard_map/all_to_all | solution.py:66
  51.0 1.2 reshape.416
  52.2 0.5 copy.13
  52.7 34.7 %all-to-all-done.3 = bf16[8,192,512]{2,1,0:T(8,128)(2,1)} async-done(((bf16[8,192,512]{2,1,0:T(8,128)(2,1)}), bf16[8,192,512]{2,1,0:T(8,128)(2,1)}, u32[]{:S(2)}, u32[]{:S(2)}) %all-to-all-start.3) | async-done | bytes 1572896 | tf_op jit(solution)/shard_map/all_to_all | solution.py:66
  87.4 2.1 tile.12
  89.5 4.6 %all-to-all-start.1 = ((bf16[8,192,1024]{2,1,0:T(8,128)(2,1)}), bf16[8,192,1024]{2,1,0:T(8,128)(2,1)}, u32[]{:S(2)}, u32[]{:S(2)}) async-start(bf16[8,192,1024]{2,1,0:T(8,128)(2,1)} %bitcast.3), calls=%async_computation.1 | async-start | bytes 6291456 | tf_op jit(solution)/shard_map/all_to_all | solution.py:65
  94.1 1.9 collective-permute-start.5
  96.0 5.8 %all_gather.7 = bf16[256,512]{1,0:T(8,128)(2,1)S(1)} all-gather(bf16[256,128]{1,0:T(8,128)(2,1)S(1)} %copy-done.15), channel_id=1, replica_groups=mesh['seq'=8,'head'=4] {'head'}, dimensions={1}, use_global_device_ids=true | all-gather | bytes 327680 | tf_op jit(solution)/shard_map/all_gather | solution.py:49
  101.8 0.2 collective-permute-start.2
  102.0 8.6 %all_gather.6 = bf16[256,1536]{1,0:T(8,128)(2,1)S(1)} all-gather(bf16[256,384]{1,0:T(8,128)(2,1)S(1)} %copy-done.14), channel_id=1, replica_groups=mesh['seq'=8,'head'=4] {'head'}, dimensions={1}, use_global_device_ids=true | all-gather | bytes 983040 | tf_op jit(solution)/shard_map/all_gather | solution.py:48
  110.6 1.8 collective-permute-start
  112.6 15.3 %collective-permute-done.2 = bf16[256,512]{1,0:T(8,128)(2,1)S(1)} collective-permute-done((bf16[256,512]{1,0:T(8,128)(2,1)S(1)}, bf16[256,512]{1,0:T(8,128)(2,1)S(1)}, u32[]{:S(2)}, u32[]{:S(2)}) %collective-permute-start.2) | collective-permute-done | bytes 262176 | tf_op jit(solution)/shard_map/ppermute | solution.py:21
  128.0 0.2 maximum_select_fusion.5
  128.3 0.1 fusion.40
  128.4 0.1 pad_dynamic-slice_fusion.7
  128.5 0.6 and_and_fusion.1
  129.1 27.2 %collective-permute-done.3 = bf16[512,512]{1,0:T(8,128)(2,1)S(1)} collective-permute-done((bf16[512,512]{1,0:T(8,128)(2,1)S(1)}, bf16[512,512]{1,0:T(8,128)(2,1)S(1)}, u32[]{:S(2)}, u32[]{:S(2)}) %collective-permute-start.3) | collective-permute-done | bytes 524320 | tf_op jit(solution)/shard_map/ppermute | solution.py:21
  156.3 0.5 maximum_select_fusion.2
  156.8 6.0 %collective-permute-start.4 = (bf16[768,512]{1,0:T(8,128)(2,1)S(1)}, bf16[768,512]{1,0:T(8,128)(2,1)S(1)}, u32[]{:S(2)}, u32[]{:S(2)}) collective-permute-start(bf16[768,512]{1,0:T(8,128)(2,1)S(1)} %slice.117), channel_id=1, source_target_pairs={{0,16},{4,20},{8,24},{12,28},{1,17},{5,21},{9,25},{13,29},{2,18},{... | collective-permute-start | bytes 2359304 | tf_op jit(solution)/shard_map/ppermute | solution.py:27
  162.8 0.6 maximum_select_fusion.1
  163.5 0.3 and_and_fusion.3
  163.9 2.1 collective-permute-start.6
  165.9 0.3 and_and_fusion
  166.3 46.8 %collective-permute-done.6 = bf16[512,64]{0,1:T(8,128)(2,1)S(1)} collective-permute-done((bf16[512,64]{0,1:T(8,128)(2,1)S(1)}, bf16[512,64]{0,1:T(8,128)(2,1)S(1)}, u32[]{:S(2)}, u32[]{:S(2)}) %collective-permute-start.6) | collective-permute-done | bytes 65568 | tf_op jit(solution)/shard_map/ppermute | solution.py:21
  213.1 0.6 slice.119
  213.7 6.0 %collective-permute-start.7 = (bf16[768,64]{0,1:T(8,128)(2,1)}, bf16[768,64]{0,1:T(8,128)(2,1)}, u32[]{:S(2)}, u32[]{:S(2)}) collective-permute-start(bf16[768,64]{0,1:T(8,128)(2,1)} %slice.119), channel_id=1, source_target_pairs={{0,16},{4,20},{8,24},{12,28},{1,17},{5,21},{9,25},{13,29},{2,18},{... | collective-permute-start | bytes 294920 | tf_op jit(solution)/shard_map/ppermute | solution.py:27
  219.7 2.2 multiply_convert_fusion
  221.9 2.9 %fusion.37 = (bf16[1024,1024]{0,1:T(8,128)(2,1)}, bf16[1024,1024]{0,1:T(8,128)(2,1)}, bf16[1024,1024]{0,1:T(8,128)(2,1)}, bf16[1024,1024]{0,1:T(8,128)(2,1)S(1)}) fusion(bf16[1792,1024]{0,1:T(8,128)(2,1)S(1)} %multiply_convert_fusion), kind=kLoop, calls=%fused_computation.82 | loop fusion | bytes 16777216 | tf_op jit(solution)/shard_map/slice | solution.py:131
  224.8 3.9 %multiply_convert_fusion.3 = bf16[1024,512]{0,1:T(8,128)(2,1)S(1)} fusion(bf16[1536,512]{1,0:T(8,128)(2,1)} %bitcast.13, bf16[512,1536]{1,0:T(8,128)(2,1)S(1)} %maximum_select_fusion.1, bf16[512,1536]{1,0:T(8,128)(2,1)S(1)} %collective-permute-done.1, pred[]{:T(512)S(6)} %eq.82), kind=kOutput, calls=%fused_computation.20 | convolution fusion | flops 1625817088 | bytes 5767169 | tf_op jit(solution)/shard_map/dot_general | solution.py:105
  228.7 0.9 fusion.39
  229.7 7.2 %multiply_convert_fusion.1 = bf16[1024,1024]{0,1:T(8,128)(2,1)S(1)} fusion(bf16[1536,1024]{1,0:T(8,128)(2,1)} %bitcast.4, bf16[512,1536]{1,0:T(8,128)(2,1)} %copy-done.8, bf16[512,1536]{1,0:T(8,128)(2,1)} %copy-done.18, pred[]{:T(512)S(6)} %eq.82), kind=kOutput, calls=%fused_computation.17 | convolution fusion | flops 3237478400 | bytes 8388609 | tf_op jit(solution)/shard_map/dot_general | solution.py:100
  236.9 0.1 fusion.38
  237.1 1.4 copy-done.2
  238.5 1.3 fusion.44
  239.8 0.3 copy-done.1
  240.1 1.3 fusion.41
  241.4 0.3 copy-done
  241.7 1.3 fusion.43
  243.0 2.1 fusion.2
  245.1 1.5 fusion.42
  246.7 3.0 %fusion.11 = f32[8,256]{1,0:T(8,128)S(1)} fusion(f32[8,256,1024]{2,1,0:T(8,128)S(1)} %fusion.41, pred[256,1024]{1,0:T(8,128)(4,1)S(1)} %and_and_fusion.3, bf16[256,8,64]{0,2,1:T(8,128)(2,1)S(1)} %bitcast.108, bf16[1024,64]{0,1:T(8,128)(2,1)S(1)} %maximum_select_fusion.6, bf16[768,64]{0,1:T(8,128)(2,1)} %collective-permute-done.7), kind=kOutput, calls=%fused_computation.15 | convolution fusion | flops 277084160 | bytes 9150464 | tf_op jit(solution)/shard_map/qhd,kd->hqk/dot_general | solution.py:32
  249.7 2.9 %fusion.5 = f32[8,256]{1,0:T(8,128)S(1)} fusion(f32[8,256,1024]{2,1,0:T(8,128)S(1)} %fusion.43, pred[256,1024]{1,0:T(8,128)(4,1)S(1)} %get-tuple-element.29, bf16[256,8,64]{0,2,1:T(8,128)(2,1)S(1)} %bitcast.107, bf16[1024,64]{0,1:T(8,128)(2,1)S(1)} %maximum_select_fusion.6, bf16[768,64]{0,1:T(8,128)(2,1)} %collective-permute-done.7), kind=kOutput, calls=%fused_computation.7 | convolution fusion | flops 277084160 | bytes 9150464 | tf_op jit(solution)/shard_map/qhd,kd->hqk/dot_general | solution.py:32
  252.6 3.1 %fusion.8 = f32[8,256]{1,0:T(8,128)S(1)} fusion(f32[8,256,1024]{2,1,0:T(8,128)S(1)} %fusion.42, pred[256,1024]{1,0:T(8,128)(4,1)S(1)} %get-tuple-element.30, bf16[256,8,64]{0,2,1:T(8,128)(2,1)S(1)} %bitcast.106, bf16[1024,64]{0,1:T(8,128)(2,1)S(1)} %maximum_select_fusion.6, bf16[768,64]{0,1:T(8,128)(2,1)} %collective-permute-done.7), kind=kOutput, calls=%fused_computation.11 | convolution fusion | flops 277084160 | bytes 9150464 | tf_op jit(solution)/shard_map/qhd,kd->hqk/dot_general | solution.py:32
  255.8 0.8 collective-permute-start.8
  256.5 3.2 %collective-permute-done.8 = f32[1,4,8,256]{3,2,0,1:T(8,128)S(1)} collective-permute-done((f32[1,4,8,256]{3,2,0,1:T(8,128)S(1)}, f32[1,4,8,256]{3,2,0,1:T(8,128)S(1)}, u32[]{:S(2)}, u32[]{:S(2)}) %collective-permute-start.8) | collective-permute-done | bytes 32800 | tf_op jit(solution)/shard_map/ppermute | solution.py:21
  259.8 2.6 collective-permute-start.9
  263.0 1.6 collective-permute-done.9
  264.6 0.6 fusion.35
  265.2 0.1 reduce_max.52
  265.3 17.8 %pmax.7 = f32[32]{0:T(128)S(1)} all-reduce(f32[32]{0:T(128)S(1)} %reduce_max.52), channel_id=1, replica_groups=mesh['seq'=8,'head'=4] {'seq'}, use_global_device_ids=true, to_apply=%region_5.6 | all-reduce | flops 32 | bytes 256 | tf_op jit(solution)/shard_map/pmax | solution.py:146
  283.2 0.9 multiply_convert_fusion.5
  284.1 1.5 multiply_convert_fusion.2
  285.7 1.0 multiply_convert_fusion.4
  (64 shorter events, 0.7 us)
Async XLA Ops:
  0.6 19.8 %copy-start.5 = (bf16[192,2048]{1,0:T(8,128)(2,1)S(1)}, bf16[192,2048]{1,0:T(8,128)(2,1)}, u32[]{:S(2)}) copy-start(bf16[192,2048]{1,0:T(8,128)(2,1)} %param.13) | copy-start | bytes 2359300
  2.0 13.8 %all-to-all-start = ((s32[8,1,256]{2,1,0:T(1,128)}), s32[8,1,256]{2,1,0:T(1,128)S(1)}, u32[]{:S(2)}, u32[]{:S(2)}) async-start(s32[8,1,256]{2,1,0:T(1,128)} %stack.12), calls=%async_computation | async-start | bytes 16384 | tf_op jit(solution)/shard_map/all_to_all | solution.py:111
  16.9 28.3 %all-to-all-start.2 = ((bf16[8,64,1024]{2,1,0:T(8,128)(2,1)}), bf16[8,64,1024]{2,1,0:T(8,128)(2,1)S(1)}, u32[]{:S(2)}, u32[]{:S(2)}) async-start(bf16[8,64,1024]{2,1,0:T(8,128)(2,1)} %bitcast.7), calls=%async_computation.2 | async-start | bytes 2097152 | tf_op jit(solution)/shard_map/all_to_all | solution.py:67
  21.2 29.8 %copy-start.3 = (bf16[192,4096]{1,0:T(8,128)(2,1)S(1)}, bf16[192,4096]{1,0:T(8,128)(2,1)}, u32[]{:S(2)}) copy-start(bf16[192,4096]{1,0:T(8,128)(2,1)} %param.12) | copy-start | bytes 4718596
  45.2 1.5 copy-start.9
  46.7 40.7 %all-to-all-start.3 = ((bf16[8,192,512]{2,1,0:T(8,128)(2,1)}), bf16[8,192,512]{2,1,0:T(8,128)(2,1)}, u32[]{:S(2)}, u32[]{:S(2)}) async-start(bf16[8,192,512]{2,1,0:T(8,128)(2,1)} %bitcast.12), calls=%async_computation.3 | async-start | bytes 3145728 | tf_op jit(solution)/shard_map/all_to_all | solution.py:66
  89.5 4.6 %copy-start.16 = (bf16[256,64]{0,1:T(8,128)(2,1)S(1)}, bf16[256,64]{0,1:T(8,128)(2,1)}, u32[]{:S(2)}) copy-start(bf16[256,64]{0,1:T(8,128)(2,1)} %param.10) | copy-start | bytes 98308
  89.5 6.5 %copy-start.15 = (bf16[256,128]{1,0:T(8,128)(2,1)S(1)}, bf16[256,128]{1,0:T(8,128)(2,1)}, u32[]{:S(2)}) copy-start(bf16[256,128]{1,0:T(8,128)(2,1)} %param.9) | copy-start | bytes 196612
  89.5 12.5 %copy-start.14 = (bf16[256,384]{1,0:T(8,128)(2,1)S(1)}, bf16[256,384]{1,0:T(8,128)(2,1)}, u32[]{:S(2)}) copy-start(bf16[256,384]{1,0:T(8,128)(2,1)} %param.8) | copy-start | bytes 589828
  89.5 140.1 %all-to-all-start.1 = ((bf16[8,192,1024]{2,1,0:T(8,128)(2,1)}), bf16[8,192,1024]{2,1,0:T(8,128)(2,1)}, u32[]{:S(2)}, u32[]{:S(2)}) async-start(bf16[8,192,1024]{2,1,0:T(8,128)(2,1)} %bitcast.3), calls=%async_computation.1 | async-start | bytes 6291456 | tf_op jit(solution)/shard_map/all_to_all | solution.py:65
  94.1 69.7 %collective-permute-start.5 = (bf16[256,64]{0,1:T(8,128)(2,1)S(1)}, bf16[256,64]{0,1:T(8,128)(2,1)S(1)}, u32[]{:S(2)}, u32[]{:S(2)}) collective-permute-start(bf16[256,64]{0,1:T(8,128)(2,1)S(1)} %copy-done.16), channel_id=1, source_target_pairs={{0,4},{4,0},{8,12},{12,8},{16,20},{20,16},{24,28},{28,24},{1,5},{5... | collective-permute-start | bytes 98312 | tf_op jit(solution)/shard_map/ppermute | solution.py:21
  101.8 26.1 %collective-permute-start.2 = (bf16[256,512]{1,0:T(8,128)(2,1)S(1)}, bf16[256,512]{1,0:T(8,128)(2,1)S(1)}, u32[]{:S(2)}, u32[]{:S(2)}) collective-permute-start(bf16[256,512]{1,0:T(8,128)(2,1)S(1)} %all_gather.7), channel_id=1, source_target_pairs={{0,4},{4,0},{8,12},{12,8},{16,20},{20,16},{24,28},{28,24},{1,5},{5... | collective-permute-start | bytes 786440 | tf_op jit(solution)/shard_map/ppermute | solution.py:21
  110.6 52.2 %collective-permute-start = (bf16[256,1536]{1,0:T(8,128)(2,1)S(1)}, bf16[256,1536]{1,0:T(8,128)(2,1)S(1)}, u32[]{:S(2)}, u32[]{:S(2)}) collective-permute-start(bf16[256,1536]{1,0:T(8,128)(2,1)S(1)} %all_gather.6), channel_id=1, source_target_pairs={{0,4},{4,0},{8,12},{12,8},{16,20},{20,16},{24,28},{28,24},{1,5},{5... | collective-permute-start | bytes 2359304 | tf_op jit(solution)/shard_map/ppermute | solution.py:21
  128.2 28.1 %collective-permute-start.3 = (bf16[512,512]{1,0:T(8,128)(2,1)S(1)}, bf16[512,512]{1,0:T(8,128)(2,1)S(1)}, u32[]{:S(2)}, u32[]{:S(2)}) collective-permute-start(bf16[512,512]{1,0:T(8,128)(2,1)S(1)} %maximum_select_fusion.5), channel_id=1, source_target_pairs={{0,8},{4,12},{8,0},{12,4},{16,24},{20,28},{24,16},{28,20},{1,9},{5... | collective-permute-start | bytes 1572872 | tf_op jit(solution)/shard_map/ppermute | solution.py:21
  156.7 63.0 %copy-start.10 = (bf16[8,64,1024]{2,1,0:T(8,128)(2,1)S(1)}, bf16[8,64,1024]{2,1,0:T(8,128)(2,1)}, u32[]{:S(2)}) copy-start(bf16[8,64,1024]{2,1,0:T(8,128)(2,1)} %copy-done.9) | copy-start | bytes 3145732
  156.8 62.9 %collective-permute-start.4 = (bf16[768,512]{1,0:T(8,128)(2,1)S(1)}, bf16[768,512]{1,0:T(8,128)(2,1)S(1)}, u32[]{:S(2)}, u32[]{:S(2)}) collective-permute-start(bf16[768,512]{1,0:T(8,128)(2,1)S(1)} %slice.117), channel_id=1, source_target_pairs={{0,16},{4,20},{8,24},{12,28},{1,17},{5,21},{9,25},{13,29},{2,18},{... | collective-permute-start | bytes 2359304 | tf_op jit(solution)/shard_map/ppermute | solution.py:27
  163.4 61.4 %copy-start.8 = (bf16[512,1536]{1,0:T(8,128)(2,1)}, bf16[512,1536]{1,0:T(8,128)(2,1)S(1)}, u32[]{:S(2)}) copy-start(bf16[512,1536]{1,0:T(8,128)(2,1)S(1)} %maximum_select_fusion.1) | copy-start | bytes 4718596
  163.4 61.4 %collective-permute-start.1 = (bf16[512,1536]{1,0:T(8,128)(2,1)S(1)}, bf16[512,1536]{1,0:T(8,128)(2,1)S(1)}, u32[]{:S(2)}, u32[]{:S(2)}) collective-permute-start(bf16[512,1536]{1,0:T(8,128)(2,1)S(1)} %maximum_select_fusion.1), channel_id=1, source_target_pairs={{0,8},{4,12},{8,0},{12,4},{16,24},{20,28},{24,16},{28,20},{1,9},{5... | collective-permute-start | bytes 4718600 | tf_op jit(solution)/shard_map/ppermute | solution.py:21
  163.9 49.2 %collective-permute-start.6 = (bf16[512,64]{0,1:T(8,128)(2,1)S(1)}, bf16[512,64]{0,1:T(8,128)(2,1)S(1)}, u32[]{:S(2)}, u32[]{:S(2)}) collective-permute-start(bf16[512,64]{0,1:T(8,128)(2,1)S(1)} %maximum_select_fusion.7), channel_id=1, source_target_pairs={{0,8},{4,12},{8,0},{12,4},{16,24},{20,28},{24,16},{28,20},{1,9},{5... | collective-permute-start | bytes 196616 | tf_op jit(solution)/shard_map/ppermute | solution.py:21
  213.7 32.9 %collective-permute-start.7 = (bf16[768,64]{0,1:T(8,128)(2,1)}, bf16[768,64]{0,1:T(8,128)(2,1)}, u32[]{:S(2)}, u32[]{:S(2)}) collective-permute-start(bf16[768,64]{0,1:T(8,128)(2,1)} %slice.119), channel_id=1, source_target_pairs={{0,16},{4,20},{8,24},{12,28},{1,17},{5,21},{9,25},{13,29},{2,18},{... | collective-permute-start | bytes 294920 | tf_op jit(solution)/shard_map/ppermute | solution.py:27
  224.8 3.9 %copy-start.18 = (bf16[512,1536]{1,0:T(8,128)(2,1)}, bf16[512,1536]{1,0:T(8,128)(2,1)S(1)}, u32[]{:S(2)}) copy-start(bf16[512,1536]{1,0:T(8,128)(2,1)S(1)} %collective-permute-done.1) | copy-start | bytes 4718596
  236.9 1.6 copy-start.2
  238.5 1.6 copy-start.1
  240.1 1.6 copy-start
  241.7 1.3 copy-start.13
  245.1 1.5 copy-start.12
  246.7 3.1 %copy-start.11 = (bf16[256,512]{0,1:T(8,128)(2,1)S(1)}, bf16[256,512]{0,1:T(8,128)(2,1)}, u32[]{:S(2)}) copy-start(bf16[256,512]{0,1:T(8,128)(2,1)} %get-tuple-element.19) | copy-start | bytes 786436
  252.6 30.6 %copy-start.7 = (bf16[64,4096]{1,0:T(8,128)(2,1)S(1)}, bf16[64,4096]{1,0:T(8,128)(2,1)}, u32[]{:S(2)}) copy-start(bf16[64,4096]{1,0:T(8,128)(2,1)} %param.14) | copy-start | bytes 1572868
  252.6 31.4 %copy-start.4 = (bf16[192,4096]{1,0:T(8,128)(2,1)S(1)}, bf16[192,4096]{1,0:T(8,128)(2,1)}, u32[]{:S(2)}) copy-start(bf16[192,4096]{1,0:T(8,128)(2,1)} %param.12) | copy-start | bytes 4718596
  255.8 29.9 %copy-start.6 = (bf16[192,2048]{1,0:T(8,128)(2,1)S(1)}, bf16[192,2048]{1,0:T(8,128)(2,1)}, u32[]{:S(2)}) copy-start(bf16[192,2048]{1,0:T(8,128)(2,1)} %param.13) | copy-start | bytes 2359300
  255.8 4.0 %collective-permute-start.8 = (f32[1,4,8,256]{3,2,0,1:T(8,128)S(1)}, f32[1,4,8,256]{3,2,0,1:T(8,128)S(1)}, u32[]{:S(2)}, u32[]{:S(2)}) collective-permute-start(f32[1,4,8,256]{3,2,0,1:T(8,128)S(1)} %maximum_bitcast_fusion), channel_id=1, source_target_pairs={{0,4},{4,0},{8,12},{12,8},{16,20},{20,16},{24,28},{28,24},{1,5},{5... | collective-permute-start | bytes 98312 | tf_op jit(solution)/shard_map/ppermute | solution.py:21
  259.8 4.8 %collective-permute-start.9 = (f32[2,4,8,256]{3,2,0,1:T(8,128)S(1)}, f32[2,4,8,256]{3,2,0,1:T(8,128)S(1)}, u32[]{:S(2)}, u32[]{:S(2)}) collective-permute-start(f32[2,4,8,256]{3,2,0,1:T(8,128)S(1)} %maximum_select_fusion.8), channel_id=1, source_target_pairs={{0,8},{4,12},{8,0},{12,4},{16,24},{20,28},{24,16},{28,20},{1,9},{5... | collective-permute-start | bytes 196616 | tf_op jit(solution)/shard_map/ppermute | solution.py:21
  283.1 3.6 %copy-start.17 = (f32[32]{0:T(128)}, f32[32]{0:T(128)S(1)}, u32[]{:S(2)}) copy-start(f32[32]{0:T(128)S(1)} %pmax.7) | copy-start | bytes 388
